TPU v7x, 32 devices: a whole 2x2x4 slice. The times are simulated.
32 devices in a mesh: section: 2 (over core), dp: 16 (over z, y, x).
Axes of the slice: x: 2, y: 2, z: 4, core: 2. Of those that a mesh axis runs over, the one named last changes fastest.
Arguments:
- tokens: bfloat16 [2, 16, 80, 1024], P(None, 'dp'), may hold values from -6 to 6
- w_qkv: bfloat16 [2, 1024, 1536], P('section', 'dp'), may hold values from -0.1875 to 0.1875
- w_output: bfloat16 [2, 512, 1024], P('section', None, 'dp'), may hold values from -0.25 to 0.25
- tangent_value: bfloat16 [2, 2, 1024, 512], P('section', None, 'dp'), may hold values from -0.1875 to 0.1875
- tangent_output: bfloat16 [2, 2, 512, 1024], P('section', None, None, 'dp'), may hold values from -0.25 to 0.25
- layer_gain: float32 [2, 1024], P('section'), may hold values from 0.5 to 1.5
- final_gain: float32 [1024], replicated, may hold values from 0.5 to 1.5
- head: bfloat16 [1024, 1000], P(None, 'section'), may hold values from -0.1875 to 0.1875
Outputs:
- mean_logits: float32 [2, 16, 1000], P(None, 'dp', 'section')
- variance: float32 [2, 16, 1000], P(None, 'dp', 'section')
All inputs are finite; a program needn't handle non-finite values.
Results may differ from a plain program's by a relative error of at most 0.018.
Values may be sent and summed in bfloat16 or wider, within the bound.
A program may use at most 64 MiB of HBM per device.

v0:
```python
import jax
import jax.numpy as jnp
from jax import lax
from jax.sharding import PartitionSpec as P

HEADS = 8
HEAD = 64
TANGENTS = 2
HD = 512
epsilon = 1e-06


def passed_along(block, axis, distance):
    devices = range(lax.axis_size(axis))
    route = [(i - distance, i) for i in devices if i - distance in devices]
    return lax.ppermute(block, axis, route)


def spread(shard, axis, root):
    mine = lax.axis_index(axis) == root
    return lax.psum(jnp.where(mine, shard, jnp.zeros_like(shard)), axis)


def contract(spec, left, right):
    return jnp.einsum(spec, left, right, preferred_element_type=jnp.float32)


def norm_jvp(primal, tangents, gains):
    average = jnp.mean(primal, -1, keepdims=True)
    centred = primal - average
    inverse = lax.rsqrt(jnp.mean(centred * centred, -1, keepdims=True) + epsilon)
    dcentred = tangents - jnp.mean(tangents, -1, keepdims=True)
    dinverse = -(inverse**3) * jnp.mean(centred * dcentred, -1, keepdims=True)
    return (centred * inverse * gains, (dcentred * inverse + centred * dinverse) * gains)


def layer_step(state, qkv_weight, out_weight, value_tangent, out_tangent, gains):
    resid = state.astype(jnp.float32)
    normed_zero, normed_rest = norm_jvp(resid[0], resid[1:], gains)
    normed = jnp.concatenate([normed_zero[None], normed_rest]).astype(jnp.bfloat16)
    streams, batch, tokens_here, width = normed.shape
    projected = contract("sbtd,de->sbte", normed, qkv_weight)
    extra_value = contract("btd,kde->kbte", normed[0], value_tangent)
    queries = projected[..., :HD]
    key_rows = projected[..., HD : 2 * HD]
    values = projected[..., 2 * HD :]
    values = jnp.concatenate([values[:1], values[1:] + extra_value])
    shape_heads = (streams, batch, tokens_here, HEADS, HEAD)
    queries = queries.astype(jnp.bfloat16).reshape(shape_heads)
    key_rows = key_rows.astype(jnp.bfloat16).reshape(shape_heads)
    values = values.astype(jnp.bfloat16).reshape(shape_heads)
    factor = HEAD ** (-0.5)
    scores = contract("bqhe,bkhe->bhqk", queries[0], key_rows[0]) * factor
    probs = jax.nn.softmax(scores, -1)
    dscores = (
        contract("sbqhe,bkhe->sbhqk", queries[1:], key_rows[0])
        + contract("bqhe,sbkhe->sbhqk", queries[0], key_rows[1:])
    ) * factor
    dprobs = probs * (dscores - jnp.sum(probs * dscores, -1, keepdims=True))
    probs_low = probs.astype(jnp.bfloat16)
    dprobs_low = dprobs.astype(jnp.bfloat16)
    attended_zero = contract("bhqk,bkhe->bqhe", probs_low, values[0])
    attended_rest = contract("sbhqk,bkhe->sbqhe", dprobs_low, values[0]) + contract(
        "bhqk,sbkhe->sbqhe", probs_low, values[1:]
    )
    attended = jnp.concatenate([attended_zero[None], attended_rest]).astype(jnp.bfloat16)
    attended = attended.reshape(streams, batch, tokens_here, HD)
    output = contract("sbte,ed->sbtd", attended, out_weight)
    extra_out = contract("bte,ked->kbtd", attended[0], out_tangent)
    output = jnp.concatenate([output[:1], output[1:] + extra_out])
    return (resid + output).astype(jnp.bfloat16)


def shards(tokens, w_qkv, w_output, tangent_value, tangent_output, layer_gain, final_gain, head):
    full_qkv, full_output, full_value_tan, full_output_tan = (
        lax.all_gather(w_qkv, "dp", axis=1, tiled=True),
        lax.all_gather(w_output, "dp", axis=2, tiled=True),
        lax.all_gather(tangent_value, "dp", axis=2, tiled=True),
        lax.all_gather(tangent_output, "dp", axis=3, tiled=True),
    )
    section_gain = layer_gain[0]

    def advance_layer(state):
        return layer_step(
            state, full_qkv[0], full_output[0], full_value_tan[0], full_output_tan[0], section_gain
        )

    def blank_layer(state):
        return jnp.zeros_like(state)

    section_index = lax.axis_index("section")
    section_count = lax.axis_size("section")
    micro_count = tokens.shape[0]
    image_tokens = tokens.shape[2]
    model_width = tokens.shape[3]
    flat_tokens = tokens.reshape(micro_count, image_tokens, model_width)
    entering = jnp.concatenate(
        [
            flat_tokens[None],
            jnp.zeros((TANGENTS, micro_count, image_tokens, model_width), jnp.bfloat16),
        ]
    )

    def advance(step, outgoing):
        incoming = passed_along(outgoing, "section", 1)
        source = jnp.where(step == 0, entering, incoming)
        return lax.cond(section_index == step, advance_layer, blank_layer, source)

    finished = lax.fori_loop(0, section_count, advance, jnp.zeros_like(entering))
    collected = finished[:, :, 0, :]
    features = spread(collected, "section", section_count - 1)
    widened = features.astype(jnp.float32)
    final_zero, final_rest = norm_jvp(widened[0], widened[1:], final_gain)
    normed_final = jnp.concatenate([final_zero[None], final_rest]).astype(jnp.bfloat16)
    logits = contract("sbd,dc->sbc", normed_final, head)
    mean_logits = logits[0][:, None, :]
    variance = jnp.sum(logits[1:] * logits[1:], 0)[:, None, :]
    return (mean_logits, variance)


def solution(mesh):
    return jax.shard_map(
        shards,
        mesh=mesh,
        in_specs=(
            P(None, "dp", None, None),
            P("section", "dp", None),
            P("section", None, "dp"),
            P("section", None, "dp", None),
            P("section", None, None, "dp"),
            P("section", None),
            P(),
            P(None, "section"),
        ),
        out_specs=(P(None, "dp", "section"), P(None, "dp", "section")),
        check_vma=False,
    )
```

profile of v0, /device:TPU:0, one launch (start us, length us, event | category | flops | bytes accessed | tf_op | source)
XLA Modules:
  0.0 363.6 jit_solution(397658022795245036)
XLA Ops:
  7.2 0.7 all-gather.9.cloned.1.call-update
  8.0 1.7 copy.64
  9.8 0.7 all-gather.7.cloned.1.call-update
  10.5 0.5 all-gather.5.cloned.1.call-update
  11.0 2.1 concatenate.31
  13.1 55.5 %all-gather.9.cloned.1.call-done = bf16[1,512,1024]{1,2,0:T(8,128)(2,1)} async-done(((bf16[1,512,64]{1,2,0:T(8,128)(2,1)}), bf16[1,512,1024]{1,2,0:T(8,128)(2,1)}) %all-gather.9.cloned.1.call-update) | async-done | bytes 1048592 | tf_op jit(solution)/shard_map/all_gather | solution.py:77
  68.6 2.3 copy.65
  70.9 59.7 %all-gather.11.cloned.1.call-done = bf16[1,2,512,1024]{2,1,0,3:T(2,128)(2,1)} async-done(((bf16[1,2,512,64]{2,1,0,3:T(2,128)(2,1)}), bf16[1,2,512,1024]{2,1,0,3:T(2,128)(2,1)}) %all-gather.11.cloned.1.call-update) | async-done | bytes 2097168 | tf_op jit(solution)/shard_map/all_gather | solution.py:79
  130.6 6.2 %copy.66 = bf16[1,2,512,1024]{3,2,1,0:T(8,128)(2,1)} copy(bf16[1,2,512,1024]{2,1,0,3:T(2,128)(2,1)} %all-gather.11.cloned.1.call-done) | data formatting | bytes 4194304 | tf_op jit(solution)/shard_map/while | solution.py:109
  136.8 55.8 %all-gather.7.cloned.1.call-done = bf16[1,2,1024,512]{3,2,1,0:T(8,128)(2,1)} async-done(((bf16[1,2,64,512]{3,2,1,0:T(8,128)(2,1)}), bf16[1,2,1024,512]{3,2,1,0:T(8,128)(2,1)}) %all-gather.7.cloned.1.call-update) | async-done | bytes 2097168 | tf_op jit(solution)/shard_map/all_gather | solution.py:78
  192.5 69.3 %all-gather.5.cloned.1.call-done = bf16[1,1024,1536]{2,1,0:T(8,128)(2,1)} async-done(((bf16[1,64,1536]{2,1,0:T(8,128)(2,1)}), bf16[1,1024,1536]{2,1,0:T(8,128)(2,1)}) %all-gather.5.cloned.1.call-update) | async-done | bytes 3145744 | tf_op jit(solution)/shard_map/all_gather | solution.py:76
  261.8 1.1 broadcast.171
  262.9 47.7 %while.13 = (s32[]{:T(128)}, bf16[3,2,80,1024]{3,2,1,0:T(8,128)(2,1)}, s32[]{:T(128)}, bf16[3,2,80,1024]{3,2,1,0:T(8,128)(2,1)}, f32[1,1024]{1,0:T(1,128)S(1)}, ...) while((s32[]{:T(128)}, ...), condition=%wide.region_10.11_spmd, body=%wide.region_0.10_spmd.sunk | while | flops 2827160064 | bytes 100394192 | solution.py:109
  262.9 1.3 collective-permute-start
  264.2 2.3 collective-permute-done
  266.5 39.3 %conditional.2 = (bf16[3,2,80,1024]{3,2,1,0:T(8,128)(2,1)}) conditional(s32[]{:T(128)} %convert_element_type.51, () %tuple.55, (s32[]{:T(128)}, bf16[3,2,80,1024]{3,2,1,0:T(8,128)(2,1)}, bf16[3,2,80,1024]{3,2,1,0:T(8,128)(2,1)S(1)}, f32[1,1024]{1,0:T(1,128)S(1)}, bf16[1,1024,1536]{2,1,0:T(8,128)(2,1)}, /*index=5*/bf16[1,2,1024,512]{3,2,1,0:T(8,128)(2,1)}, ...), branch_computations={%region_1.1_spmd, %region_2.9_spmd} | conditional | flops 2827160064 | bytes 96461808 | solution.py:107
  266.5 0.9 copy-done.7
  267.5 1.3 select_convert_fusion
  270.3 1.2 copy-done.10
  271.5 2.9 fusion.83
  274.4 0.5 fusion.25
  274.9 1.2 slice.90
  276.0 1.1 fusion.82
  277.2 1.9 fusion.81
  279.1 0.9 squeeze.39
  280.0 0.9 squeeze.40
  281.2 2.2 slice.87
  283.4 2.2 slice.85
  285.6 2.9 convolution_bitcast_fusion.1
  288.5 2.3 fusion.84
  290.8 1.3 broadcast_multiply_fusion
  292.5 1.4 multiply_reduce_fusion
  294.3 0.7 copy-done.3
  295.0 1.2 fusion.17
  296.2 1.0 convolution_convert_fusion
  297.2 2.2 copy.61
  299.4 2.2 concatenate.26
  301.8 2.1 fusion.28
  304.0 0.5 fusion.11
  304.6 1.3 fusion.7
  305.9 1.3 collective-permute-start
  307.2 2.3 collective-permute-done
  309.5 1.1 conditional.2
  309.5 1.1 broadcast.159
  310.6 2.1 copy.67
  312.7 41.8 %psum.7 = bf16[3,2,1024]{2,0,1:T(4,128)(2,1)S(1)} all-reduce(bf16[3,2,1024]{2,0,1:T(4,128)(2,1)S(1)} %fusion.71), channel_id=1, replica_groups=mesh['section'=2,'dp'=16] {'section'}, use_global_device_ids=true, to_apply=%region_11.12 | all-reduce | flops 6144 | bytes 24576 | tf_op jit(solution)/shard_map/psum | solution.py:21
  355.8 0.6 slice_bitcast_fusion
  356.4 0.6 broadcast_in_dim.7
  (54 shorter events, 3.9 us)
Async XLA Ops:
  7.2 348.2 %copy-start = (bf16[1024,500]{0,1:T(8,128)(2,1)S(1)}, bf16[1024,500]{0,1:T(8,128)(2,1)}, u32[]{:S(2)}) copy-start(bf16[1024,500]{0,1:T(8,128)(2,1)} %param.19) | copy-start | bytes 3072004
  7.2 61.4 %all-gather.9.cloned.1.call-start = ((), (), s32[]{:S(2)}) async-start(), calls=%async_computation.2 | async-start | bytes 1114112 | tf_op jit(solution)/shard_map/all_gather | solution.py:77
  7.9 122.7 %all-gather.11.cloned.1.call-start = ((), (), s32[]{:S(2)}) async-start(), calls=%async_computation.3 | async-start | bytes 2228224 | tf_op jit(solution)/shard_map/all_gather | solution.py:79
  9.7 182.8 %all-gather.7.cloned.1.call-start = ((), (), s32[]{:S(2)}) async-start(), calls=%async_computation.1 | async-start | bytes 2228224 | tf_op jit(solution)/shard_map/all_gather | solution.py:78
  10.4 251.4 %all-gather.5.cloned.1.call-start = ((), (), s32[]{:S(2)}) async-start(), calls=%async_computation | async-start | bytes 3342336 | tf_op jit(solution)/shard_map/all_gather | solution.py:76
  70.9 192.0 %copy-start.8 = (f32[1,1024]{1,0:T(1,128)S(1)}, f32[1,1024]{1,0:T(1,128)}, u32[]{:S(2)}) copy-start(f32[1,1024]{1,0:T(1,128)} %param.17) | copy-start | bytes 12292
  262.9 3.7 %collective-permute-start = (bf16[3,2,80,1024]{3,2,1,0:T(8,128)(2,1)}, bf16[3,2,80,1024]{3,2,1,0:T(8,128)(2,1)S(1)}, u32[]{:S(2)}, u32[]{:S(2)}) collective-permute-start(bf16[3,2,80,1024]{3,2,1,0:T(8,128)(2,1)} %get-tuple-element.322), channel_id=1, source_target_pairs={{0,16},{1,17},{2,18},{3,19},{4,20},{5,21},{6,22},{7,23},{8,24},{9,... | collective-permute-start | bytes 2949128 | tf_op jit(solution)/shard_map/while/body/eval_jaxpr/ppermute | solution.py:16
  266.5 0.9 copy-start.7
  269.6 1.9 copy-start.10
  271.5 2.9 copy-start.6
  290.8 1.5 copy-start.1
  290.8 1.7 copy-start.4
  293.9 1.1 copy-start.3
  297.2 4.5 %copy-start.5 = (bf16[2,8,64,80]{3,2,1,0:T(8,128)(2,1)S(1)}, bf16[2,8,64,80]{3,2,1,0:T(8,128)(2,1)}, u32[]{:S(2)}) copy-start(bf16[2,8,64,80]{3,2,1,0:T(8,128)(2,1)} %convolution_convert_fusion) | copy-start | bytes 491524 | tf_op jit(solution)/shard_map/while/body/eval_jaxpr/cond
  301.8 2.2 copy-start.2
  305.9 3.7 %collective-permute-start = (bf16[3,2,80,1024]{3,2,1,0:T(8,128)(2,1)}, bf16[3,2,80,1024]{3,2,1,0:T(8,128)(2,1)S(1)}, u32[]{:S(2)}, u32[]{:S(2)}) collective-permute-start(bf16[3,2,80,1024]{3,2,1,0:T(8,128)(2,1)} %get-tuple-element.322), channel_id=1, source_target_pairs={{0,16},{1,17},{2,18},{3,19},{4,20},{5,21},{6,22},{7,23},{8,24},{9,... | collective-permute-start | bytes 2949128 | tf_op jit(solution)/shard_map/while/body/eval_jaxpr/ppermute | solution.py:16
  310.6 44.4 %copy-start.9 = (f32[1024]{0:T(1024)S(1)}, f32[1024]{0:T(1024)}, u32[]{:S(2)}) copy-start(f32[1024]{0:T(1024)} %param.18) | copy-start | bytes 12292
Sparse Core Ops, SparseCore 0:
  10.7 57.7 all-gather.8
  71.4 59.2 all-gather.10
  133.4 59.1 all-gather.6
  195.2 66.5 all-gather.4
where the time goes:
time: 364 us
  waiting for transfers between devices  247 us (68%)
  blocking collectives  41.8 us (11%)
  local copies, waits for them, and re-layouts  36.2 us (10%)
  matrix products  15.6 us (4%)
  between operations  13.8 us (4%)
  other arithmetic  6.18 us (2%)
    all_gather x1, waiting for transfers between devices, shards(): lax.all_gather(w_qkv, 'dp', axis=1, tiled=True)  69.3 us
    all_gather x1, waiting for transfers between devices, shards(): lax.all_gather(tangent_output, 'dp', axis=3, tiled=True)  59.7 us
    all_gather x1, waiting for transfers between devices, shards(): lax.all_gather(tangent_value, 'dp', axis=2, tiled=True)  55.8 us
    all_gather x1, waiting for transfers between devices, shards(): lax.all_gather(w_output, 'dp', axis=2, tiled=True)  55.5 us
    psum x1, blocking collectives, spread(): return lax.psum(jnp.where(mine, shard, jnp.zeros_like(shard)), axis)  41.8 us
    dot_general x10, matrix products, contract(): return jnp.einsum(spec, left, right, preferred_element_type=jnp.float32)  13.3 us
    while x3, local copies, waits for them, and re-layouts, shards(): lax.fori_loop(0, section_count, advance, jnp.zeros_like(entering))  10.5 us
  transfers between devices with their start and end apart: 6, of which 6 were waited for; matrix products, arithmetic and copies ran while one was open for 3% of the time, Pallas kernels for 0%

commit v1 on v0

--- a/solution.py
+++ b/solution.py
@@ -2,6 +2,7 @@
 import jax.numpy as jnp
 from jax import lax
 from jax.sharding import PartitionSpec as P
+from jax.lax import all_gather
 
 HEADS = 8
 HEAD = 64
@@ -76,7 +77,7 @@
         lax.all_gather(w_qkv, "dp", axis=1, tiled=True),
         lax.all_gather(w_output, "dp", axis=2, tiled=True),
         lax.all_gather(tangent_value, "dp", axis=2, tiled=True),
-        lax.all_gather(tangent_output, "dp", axis=3, tiled=True),
+        jnp.concatenate(all_gather(tangent_output, axis_name="dp"), axis=3),
     )
     section_gain = layer_gain[0]
 

time: 364 us -> 366 us (level)
  waiting for transfers between devices: 247 us -> 255 us
  local copies, waits for them, and re-layouts: 36.2 us -> 28.7 us
    while x3 -> x2, local copies, waits for them, and re-layouts: 10.5 us -> 4.34 us  [shards(): lax.fori_loop(0, section_count, advance, jnp.zeros_like(entering))]
    all_gather x1, waiting for transfers between devices: 55.8 us -> 59.7 us  [shards(): lax.all_gather(tangent_value, 'dp', axis=2, tiled=True)]
  transfers between devices with their start and end apart: 6 -> 6, of which waited for: 6 -> 6; matrix products, arithmetic and copies ran while one was open for 3% -> 1% of each run, Pallas kernels for 0% -> 0%
where the time goes in v1:
time: 366 us; the launch traced here: 365 us
  waiting for transfers between devices  255 us (70%)
  blocking collectives  42.4 us (12%)
  local copies, waits for them, and re-layouts  28.7 us (8%)
  matrix products  16 us (4%)
  between operations  13.8 us (4%)
  other arithmetic  6.28 us (2%)
    all_gather x1, waiting for transfers between devices, shards(): lax.all_gather(w_qkv, 'dp', axis=1, tiled=True)  69.3 us
    all_gather x1, waiting for transfers between devices, shards(): all_gather(tangent_output, axis_name='dp')  61.9 us
    all_gather x1, waiting for transfers between devices, shards(): lax.all_gather(tangent_value, 'dp', axis=2, tiled=True)  59.7 us
    all_gather x1, waiting for transfers between devices, shards(): lax.all_gather(w_output, 'dp', axis=2, tiled=True)  56.6 us
    psum x1, blocking collectives, spread(): return lax.psum(jnp.where(mine, shard, jnp.zeros_like(shard)), axis)  42.4 us
    dot_general x10, matrix products, contract(): return jnp.einsum(spec, left, right, preferred_element_type=jnp.float32)  13.7 us
  transfers between devices with their start and end apart: 6, of which 6 were waited for; matrix products, arithmetic and copies ran while one was open for 1% of the time, Pallas kernels for 0%

profile of v1, /device:TPU:0, one launch (start us, length us, event | category | flops | bytes accessed | tf_op | source)
XLA Modules:
  0.0 364.9 jit_solution(17337097851367675491)
XLA Ops:
  7.2 0.7 all-gather.10.cloned.1.call-update
  8.0 0.7 all-gather.8.cloned.1.call-update
  8.7 0.7 all-gather.12.cloned.1.call-update
  9.4 0.5 all-gather.6.cloned.1.call-update
  10.0 2.0 concatenate.31
  12.0 56.6 %all-gather.10.cloned.1.call-done = bf16[1,512,1024]{1,2,0:T(8,128)(2,1)} async-done(((bf16[1,512,64]{1,2,0:T(8,128)(2,1)}), bf16[1,512,1024]{1,2,0:T(8,128)(2,1)}) %all-gather.10.cloned.1.call-update) | async-done | bytes 1048592 | tf_op jit(solution)/shard_map/all_gather | solution.py:78
  68.6 2.3 copy.67
  70.9 59.7 %all-gather.8.cloned.1.call-done = bf16[1,2,1024,512]{3,2,1,0:T(8,128)(2,1)} async-done(((bf16[1,2,64,512]{3,2,1,0:T(8,128)(2,1)}), bf16[1,2,1024,512]{3,2,1,0:T(8,128)(2,1)}) %all-gather.8.cloned.1.call-update) | async-done | bytes 2097168 | tf_op jit(solution)/shard_map/all_gather | solution.py:79
  130.5 61.9 %all-gather.12.cloned.1.call-done = bf16[16,2,512,64]{2,3,0,1:T(8,128)(2,1)} async-done(((bf16[1,2,512,64]{2,3,0,1:T(8,128)(2,1)}), bf16[16,2,512,64]{2,3,0,1:T(8,128)(2,1)}) %all-gather.12.cloned.1.call-update) | async-done | bytes 2097168 | tf_op jit(solution)/shard_map/all_gather | solution.py:80
  192.4 69.3 %all-gather.6.cloned.1.call-done = bf16[1,1024,1536]{2,1,0:T(8,128)(2,1)} async-done(((bf16[1,64,1536]{2,1,0:T(8,128)(2,1)}), bf16[1,1024,1536]{2,1,0:T(8,128)(2,1)}) %all-gather.6.cloned.1.call-update) | async-done | bytes 3145744 | tf_op jit(solution)/shard_map/all_gather | solution.py:77
  261.7 1.2 broadcast.171
  262.8 48.5 %while.13 = (s32[]{:T(128)}, bf16[3,2,80,1024]{3,2,1,0:T(8,128)(2,1)}, s32[]{:T(128)}, bf16[3,2,80,1024]{3,2,1,0:T(8,128)(2,1)}, f32[1,1024]{1,0:T(1,128)S(1)}, ...) while((s32[]{:T(128)}, ...), condition=%wide.region_10.11_spmd, body=%wide.region_0.10_spmd.sunk | while | flops 2827160064 | bytes 100394192 | solution.py:110
  262.8 1.3 collective-permute-start
  264.2 2.3 collective-permute-done
  266.5 40.0 %conditional.2 = (bf16[3,2,80,1024]{3,2,1,0:T(8,128)(2,1)}) conditional(s32[]{:T(128)} %convert_element_type.51, () %tuple.55, (s32[]{:T(128)}, bf16[3,2,80,1024]{3,2,1,0:T(8,128)(2,1)}, bf16[3,2,80,1024]{3,2,1,0:T(8,128)(2,1)S(1)}, f32[1,1024]{1,0:T(1,128)S(1)}, bf16[1,1024,1536]{2,1,0:T(8,128)(2,1)}, /*index=5*/bf16[1,2,1024,512]{3,2,1,0:T(8,128)(2,1)}, ...), branch_computations={%region_1.1_spmd, %region_2.9_spmd} | conditional | flops 2827160064 | bytes 96461808 | solution.py:108
  266.5 1.0 copy-done.7
  267.6 1.3 select_convert_fusion
  270.3 1.2 copy-done.10
  271.5 2.9 fusion.76
  274.4 0.5 fusion.18
  275.0 1.2 slice.90
  276.2 1.1 fusion.75
  277.3 1.9 fusion.74
  279.2 1.0 squeeze.36
  280.2 0.9 squeeze.37
  281.3 2.2 slice.87
  283.6 2.2 slice.85
  285.8 2.9 convolution_bitcast_fusion.2
  288.7 2.3 fusion.77
  291.0 1.3 broadcast_multiply_fusion
  292.7 1.4 multiply_reduce_fusion
  294.5 0.7 copy-done.2
  295.2 1.2 fusion.10
  296.4 1.0 convolution_convert_fusion
  297.4 2.3 copy.62
  299.7 2.2 concatenate.26
  302.1 2.1 fusion.21
  304.2 0.9 fusion.6
  305.2 1.4 fusion.5
  306.5 1.3 collective-permute-start
  307.9 2.3 collective-permute-done
  310.2 1.2 conditional.2
  310.2 1.2 broadcast.159
  311.4 2.1 copy.68
  313.5 42.4 %psum.7 = bf16[3,2,1024]{2,0,1:T(4,128)(2,1)S(1)} all-reduce(bf16[3,2,1024]{2,0,1:T(4,128)(2,1)S(1)} %fusion.64), channel_id=1, replica_groups=mesh['section'=2,'dp'=16] {'section'}, use_global_device_ids=true, to_apply=%region_11.12 | all-reduce | flops 6144 | bytes 24576 | tf_op jit(solution)/shard_map/psum | solution.py:22
  356.8 0.4 fusion.62
  357.2 0.6 slice_bitcast_fusion
  357.8 0.6 broadcast_in_dim.7
  (52 shorter events, 3.5 us)
Async XLA Ops:
  7.2 349.6 %copy-start = (bf16[1024,500]{0,1:T(8,128)(2,1)S(1)}, bf16[1024,500]{0,1:T(8,128)(2,1)}, u32[]{:S(2)}) copy-start(bf16[1024,500]{0,1:T(8,128)(2,1)} %param.19) | copy-start | bytes 3072004
  7.2 61.4 %all-gather.10.cloned.1.call-start = ((), (), s32[]{:S(2)}) async-start(), calls=%async_computation.2 | async-start | bytes 1114112 | tf_op jit(solution)/shard_map/all_gather | solution.py:78
  7.9 122.6 %all-gather.8.cloned.1.call-start = ((), (), s32[]{:S(2)}) async-start(), calls=%async_computation.1 | async-start | bytes 2228224 | tf_op jit(solution)/shard_map/all_gather | solution.py:79
  8.7 183.8 %all-gather.12.cloned.1.call-start = ((), (), s32[]{:S(2)}) async-start(), calls=%async_computation.3 | async-start | bytes 2228224 | tf_op jit(solution)/shard_map/all_gather | solution.py:80
  9.4 252.3 %all-gather.6.cloned.1.call-start = ((), (), s32[]{:S(2)}) async-start(), calls=%async_computation | async-start | bytes 3342336 | tf_op jit(solution)/shard_map/all_gather | solution.py:77
  12.0 250.8 %copy-start.8 = (f32[1,1024]{1,0:T(1,128)S(1)}, f32[1,1024]{1,0:T(1,128)}, u32[]{:S(2)}) copy-start(f32[1,1024]{1,0:T(1,128)} %param.17) | copy-start | bytes 12292
  262.8 3.7 %collective-permute-start = (bf16[3,2,80,1024]{3,2,1,0:T(8,128)(2,1)}, bf16[3,2,80,1024]{3,2,1,0:T(8,128)(2,1)S(1)}, u32[]{:S(2)}, u32[]{:S(2)}) collective-permute-start(bf16[3,2,80,1024]{3,2,1,0:T(8,128)(2,1)} %get-tuple-element.322), channel_id=1, source_target_pairs={{0,16},{1,17},{2,18},{3,19},{4,20},{5,21},{6,22},{7,23},{8,24},{9,... | collective-permute-start | bytes 2949128 | tf_op jit(solution)/shard_map/while/body/eval_jaxpr/ppermute | solution.py:17
  266.5 1.0 copy-start.7
  269.6 1.9 copy-start.10
  271.5 2.9 copy-start.6
  291.0 1.5 copy-start.1
  291.0 1.7 copy-start.3
  294.1 1.1 copy-start.2
  297.4 4.6 %copy-start.4 = (bf16[2,8,64,80]{3,2,1,0:T(8,128)(2,1)S(1)}, bf16[2,8,64,80]{3,2,1,0:T(8,128)(2,1)}, u32[]{:S(2)}) copy-start(bf16[2,8,64,80]{3,2,1,0:T(8,128)(2,1)} %convolution_convert_fusion) | copy-start | bytes 491524 | tf_op jit(solution)/shard_map/while/body/eval_jaxpr/cond
  302.1 2.2 copy-start.5
  306.5 3.7 %collective-permute-start = (bf16[3,2,80,1024]{3,2,1,0:T(8,128)(2,1)}, bf16[3,2,80,1024]{3,2,1,0:T(8,128)(2,1)S(1)}, u32[]{:S(2)}, u32[]{:S(2)}) collective-permute-start(bf16[3,2,80,1024]{3,2,1,0:T(8,128)(2,1)} %get-tuple-element.322), channel_id=1, source_target_pairs={{0,16},{1,17},{2,18},{3,19},{4,20},{5,21},{6,22},{7,23},{8,24},{9,... | collective-permute-start | bytes 2949128 | tf_op jit(solution)/shard_map/while/body/eval_jaxpr/ppermute | solution.py:17
  311.4 45.0 %copy-start.9 = (f32[1024]{0:T(1024)S(1)}, f32[1024]{0:T(1024)}, u32[]{:S(2)}) copy-start(f32[1024]{0:T(1024)} %param.18) | copy-start | bytes 12292
Sparse Core Ops, SparseCore 0:
  10.7 57.7 all-gather.9
  71.3 59.1 all-gather.7
  133.3 59.0 all-gather.11
  195.0 66.5 all-gather.5
